TPU v7x, 32 devices: a whole 2x2x4 slice. The times are simulated.
32 devices in a mesh: az: 4 (over y, x), rad: 8 (over z, core).
Axes of the slice: x: 2, y: 2, z: 4, core: 2. Of those that a mesh axis runs over, the one named last changes fastest.
Arguments:
- fields: float32 [5, 96, 32, 512], P(None, 'rad', None, 'az'), may hold values from -6 to 6
- shift: int32 [96], replicated, may hold values from 0 to 511
- fraction: float32 [96], replicated, may hold values from -0.5 to 0.5
- radial_rate: float32 [96, 32], replicated, may hold values from -0.4 to 0.4
Outputs:
- updated: float32 [5, 96, 32, 512], P(None, 'rad', None, 'az')
All inputs are finite; a program needn't handle non-finite values.
Results may differ from a plain program's by a relative error of at most 0.0003.
Values sent between devices are 32-bit elements; how exact they have to be, the bound alone decides.
A program may use at most 64 MiB of HBM per device.

v0:
```python
import jax
import jax.numpy as jnp
from jax import lax
from jax.sharding import PartitionSpec as P


def with_halo(array, sides, width):
    for axis, dim in sides:
        devices, length = (lax.axis_size(axis), array.shape[dim])
        up = [(i, (i + 1) % devices) for i in range(devices - 1)]
        down = [(j, i) for i, j in up]
        last = lax.slice_in_dim(array, length - width, length, axis=dim)
        first = lax.slice_in_dim(array, 0, width, axis=dim)
        before = lax.ppermute(last, axis, up)
        after = lax.ppermute(first, axis, down)
        array = jnp.concatenate([before, array, after], axis=dim)
    return array


def cut(values, low, count, axis):
    return lax.slice_in_dim(values, low, low + count, axis=axis)


def limited(left, right):
    steep = jnp.minimum(
        jnp.minimum(2.0 * jnp.abs(left), 2.0 * jnp.abs(right)), 0.5 * jnp.abs(left + right)
    )
    return jnp.where(left * right > 0.0, jnp.sign(left) * steep, 0.0)


def flux_change(padded, courant, axis):
    count = padded.shape[axis] - 4
    left = cut(padded, 1, count + 2, axis) - cut(padded, 0, count + 2, axis)
    right = cut(padded, 2, count + 2, axis) - cut(padded, 1, count + 2, axis)
    slope = limited(left, right)
    forward = cut(padded, 1, count + 1, axis) + 0.5 * (1.0 - courant) * cut(
        slope, 0, count + 1, axis
    )
    backward = cut(padded, 2, count + 1, axis) - 0.5 * (1.0 + courant) * cut(
        slope, 1, count + 1, axis
    )
    flux = courant * jnp.where(courant > 0.0, forward, backward)
    return cut(flux, 1, count, axis) - cut(flux, 0, count, axis)


def slice_rows(doubled, starts, length):

    def one_row(row, begin):
        return lax.dynamic_slice_in_dim(row, begin, length, axis=2)

    return jax.vmap(one_row, in_axes=(1, 0), out_axes=1)(doubled, starts)


def shards(fields, shift, fraction, radial_rate):
    rows_here = fields.shape[1]
    start = lax.axis_index("rad") * rows_here
    local_shift = lax.dynamic_slice_in_dim(shift, start, rows_here)
    local_fraction = lax.dynamic_slice_in_dim(fraction, start, rows_here)
    group = lax.axis_size("az")
    per_device = rows_here // group
    offset = lax.axis_index("az") * per_device
    row_shift = lax.dynamic_slice_in_dim(local_shift, offset, per_device)
    row_fraction = lax.dynamic_slice_in_dim(local_fraction, offset, per_device)
    block = lax.all_to_all(fields, "az", split_axis=1, concat_axis=3, tiled=True)
    cycle = block.shape[3]
    doubled = jnp.concatenate([block, block], axis=3)
    rolled = slice_rows(doubled, cycle - row_shift, cycle)
    padded = jnp.concatenate([rolled[:, :, :, -2:], rolled, rolled[:, :, :, :2]], axis=3)
    result = rolled - flux_change(padded, row_fraction[None, :, None, None], 3)
    azimuthal = lax.all_to_all(result, "az", split_axis=3, concat_axis=1, tiled=True)
    edge = jnp.zeros((1, radial_rate.shape[1]), jnp.float32)
    extended = jnp.concatenate([edge, radial_rate[:-1], edge], axis=0)
    face_rates = lax.dynamic_slice_in_dim(extended, start, rows_here + 1)
    ghosted = with_halo(azimuthal, (("rad", 1),), 2)
    return azimuthal - flux_change(ghosted, face_rates[None, :, :, None], 1)


def solution(mesh):
    placed = (P(None, "rad", None, "az"), P(), P(), P())
    return jax.shard_map(
        shards, mesh=mesh, in_specs=placed, out_specs=P(None, "rad", None, "az"), check_vma=False
    )
```

profile of v0, /device:TPU:1, one launch (start us, length us, event | category | flops | bytes accessed | tf_op | source)
XLA Modules:
  0.0 94.6 jit_solution(4504958948228859008)
XLA Ops:
  0.0 2.2 %copy.48 = f32[5,12,32,128]{3,2,0,1:T(8,128)} copy(f32[5,12,32,128]{3,2,1,0:T(8,128)} %param.4) | data formatting | bytes 1966080 | tf_op args[0]
  2.2 4.4 %all-to-all-start = ((f32[5,12,32,128]{3,2,0,1:T(8,128)}), f32[5,12,32,128]{3,2,0,1:T(8,128)S(1)}, u32[]{:S(2)}, u32[]{:S(2)}) async-start(f32[5,12,32,128]{3,2,0,1:T(8,128)} %copy.48), calls=%async_computation | async-start | bytes 1966080 | tf_op jit(solution)/shard_map/all_to_all | solution.py:64
  6.8 12.3 %all-to-all-done = f32[5,12,32,128]{3,2,0,1:T(8,128)S(1)} async-done(((f32[5,12,32,128]{3,2,0,1:T(8,128)}), f32[5,12,32,128]{3,2,0,1:T(8,128)S(1)}, u32[]{:S(2)}, u32[]{:S(2)}) %all-to-all-start) | async-done | bytes 983072 | tf_op jit(solution)/shard_map/all_to_all | solution.py:64
  19.1 0.6 copy.49
  19.7 0.4 all_to_all.29
  20.3 7.0 %copy.50 = f32[5,3,32,1024]{2,0,1,3:T(8,128)} copy(f32[5,3,32,1024]{3,2,1,0:T(8,128)S(1)} %pad_maximum_fusion) | data formatting | bytes 3932160 | tf_op jit(solution)/shard_map/concatenate | solution.py:66
  27.3 8.3 %gather_fusion = f32[3,5,32,512]{2,1,3,0:T(8,128)} fusion(f32[3,5,32,1024]{2,1,0,3:T(8,128)} %bitcast.28, s32[3]{0:T(128)S(1)} %fusion.19), kind=kCustom, calls=%fused_computation | custom fusion | bytes 1966128 | tf_op jit(solution)/shard_map/vmap()/gather | solution.py:49
  35.6 4.0 %copy.51 = f32[3,5,32,512]{3,2,0,1:T(8,128)S(1)} copy(f32[3,5,32,512]{2,1,3,0:T(8,128)} %gather_fusion) | data formatting | bytes 1966080 | tf_op jit(solution)/shard_map/vmap()/gather | solution.py:49
  39.7 1.2 %multiply_select_fusion = f32[5,3,32,514]{3,2,1,0:T(8,128)S(1)} fusion(f32[5,3,32,512]{3,2,1,0:T(8,128)S(1)} %bitcast.22, f32[5,3,32,2]{3,2,1,0:T(8,128)S(1)} %get-tuple-element.9, f32[5,3,32,2]{3,2,1,0:T(8,128)S(1)} %get-tuple-element.10), kind=kLoop, calls=%fused_computation.24 | loop fusion | flops 4934400 | bytes 1977600 | tf_op jit(solution)/shard_map/jit(_where)/select_n | solution.py:28
  40.9 0.9 fusion.3
  42.2 3.5 %copy.52 = f32[5,3,32,512]{2,1,0,3:T(4,128)} copy(f32[5,3,32,512]{3,2,1,0:T(8,128)S(1)} %fusion.17) | data formatting | bytes 1966080 | tf_op jit(solution)/shard_map/sub | solution.py:69
  45.7 5.9 %reshape.29 = f32[4,1,61440]{2,1,0:T(1,128)} reshape(f32[512,5,3,32]{3,2,1,0:T(4,128)} %bitcast.19) | data formatting | bytes 1966080
  51.7 3.8 %all-to-all-start.1 = ((f32[4,1,61440]{2,1,0:T(1,128)}), f32[4,1,61440]{2,1,0:T(1,128)S(1)}, u32[]{:S(2)}, u32[]{:S(2)}) async-start(f32[4,1,61440]{2,1,0:T(1,128)} %reshape.29), calls=%async_computation.1 | async-start | bytes 1966080 | tf_op jit(solution)/shard_map/all_to_all | solution.py:70
  55.7 12.0 %all-to-all-done.1 = f32[4,1,61440]{2,1,0:T(1,128)S(1)} async-done(((f32[4,1,61440]{2,1,0:T(1,128)}), f32[4,1,61440]{2,1,0:T(1,128)S(1)}, u32[]{:S(2)}, u32[]{:S(2)}) %all-to-all-start.1) | async-done | bytes 983072 | tf_op jit(solution)/shard_map/all_to_all | solution.py:70
  67.7 0.5 broadcast.122
  68.2 3.5 %reduce = f32[4,61440]{1,0:T(4,128)S(1)} reduce(f32[4,1,61440]{2,1,0:T(1,128)S(1)} %all-to-all-done.1, f32[]{:T(128)} %broadcast.122), dimensions={1}, to_apply=%all_to_all.30.reduce_sub_computation | reduce | bytes 1966084 | tf_op jit(solution)/shard_map/all_to_all | solution.py:70
  71.7 5.6 %reshape.30 = f32[512,5,3,32]{3,2,1,0:T(4,128)} reshape(f32[4,61440]{1,0:T(4,128)S(1)} %reduce) | data formatting | bytes 1966080
  77.3 3.7 %copy.53 = f32[5,4,3,32,128]{4,3,2,1,0:T(8,128)S(1)} copy(f32[5,4,3,32,128]{3,2,0,4,1:T(4,128)} %bitcast.20) | data formatting | bytes 1966080 | tf_op jit(solution)/shard_map/all_to_all | solution.py:70
  81.1 4.6 %collective-permute-start = (f32[5,2,32,128]{3,2,1,0:T(8,128)S(1)}, f32[5,2,32,128]{3,2,1,0:T(8,128)S(1)}, u32[]{:S(2)}, u32[]{:S(2)}) collective-permute-start(f32[5,2,32,128]{3,2,1,0:T(8,128)S(1)} %get-tuple-element.7), channel_id=1, source_target_pairs={{0,1},{1,2},{2,3},{3,4},{4,5},{5,6},{6,7},{8,9},{9,10},{10,11},{11... | collective-permute-start | bytes 491528 | tf_op jit(solution)/shard_map/ppermute | solution.py:14
  85.7 1.9 %collective-permute-start.1 = (f32[5,2,32,128]{3,2,1,0:T(8,128)S(1)}, f32[5,2,32,128]{3,2,1,0:T(8,128)S(1)}, u32[]{:S(2)}, u32[]{:S(2)}) collective-permute-start(f32[5,2,32,128]{3,2,1,0:T(8,128)S(1)} %get-tuple-element.8), channel_id=1, source_target_pairs={{1,0},{2,1},{3,2},{4,3},{5,4},{6,5},{7,6},{9,8},{10,9},{11,10},{12... | collective-permute-start | bytes 491528 | tf_op jit(solution)/shard_map/ppermute | solution.py:15
  87.9 4.4 %collective-permute-done.1 = f32[5,2,32,128]{3,2,1,0:T(8,128)S(1)} collective-permute-done((f32[5,2,32,128]{3,2,1,0:T(8,128)S(1)}, f32[5,2,32,128]{3,2,1,0:T(8,128)S(1)}, u32[]{:S(2)}, u32[]{:S(2)}) %collective-permute-start.1) | collective-permute-done | bytes 163872 | tf_op jit(solution)/shard_map/ppermute | solution.py:15
  92.3 0.7 multiply_select_fusion.1
  93.0 0.4 fusion.13
  93.4 1.2 %fusion.16 = f32[5,12,32,128]{3,2,1,0:T(8,128)} fusion(f32[5,12,32,128]{3,2,1,0:T(8,128)S(1)} %bitcast.27, f32[5,13,32,128]{3,2,1,0:T(8,128)S(1)} %fusion.13), kind=kLoop, calls=%fused_computation.43 | loop fusion | flops 491520 | bytes 3932160 | tf_op jit(solution)/shard_map/sub | solution.py:75
  (19 shorter events, 1.4 us)
Async XLA Ops:
  2.2 4.4 %copy-start.2 = (s32[96]{0:T(128)S(1)}, s32[96]{0:T(128)}, u32[]{:S(2)}) copy-start(s32[96]{0:T(128)} %param.5) | copy-start | bytes 1156
  2.2 4.5 %copy-start.1 = (f32[96]{0:T(128)S(1)}, f32[96]{0:T(128)}, u32[]{:S(2)}) copy-start(f32[96]{0:T(128)} %param.6) | copy-start | bytes 1156
  2.2 16.8 %all-to-all-start = ((f32[5,12,32,128]{3,2,0,1:T(8,128)}), f32[5,12,32,128]{3,2,0,1:T(8,128)S(1)}, u32[]{:S(2)}, u32[]{:S(2)}) async-start(f32[5,12,32,128]{3,2,0,1:T(8,128)} %copy.48), calls=%async_computation | async-start | bytes 1966080 | tf_op jit(solution)/shard_map/all_to_all | solution.py:64
  51.6 3.8 %copy-start = (f32[96,32]{0,1:T(8,128)S(1)}, f32[96,32]{0,1:T(8,128)}, u32[]{:S(2)}) copy-start(f32[96,32]{0,1:T(8,128)} %param.7) | copy-start | bytes 36868
  51.7 16.1 %all-to-all-start.1 = ((f32[4,1,61440]{2,1,0:T(1,128)}), f32[4,1,61440]{2,1,0:T(1,128)S(1)}, u32[]{:S(2)}, u32[]{:S(2)}) async-start(f32[4,1,61440]{2,1,0:T(1,128)} %reshape.29), calls=%async_computation.1 | async-start | bytes 1966080 | tf_op jit(solution)/shard_map/all_to_all | solution.py:70
  81.1 6.8 %collective-permute-start = (f32[5,2,32,128]{3,2,1,0:T(8,128)S(1)}, f32[5,2,32,128]{3,2,1,0:T(8,128)S(1)}, u32[]{:S(2)}, u32[]{:S(2)}) collective-permute-start(f32[5,2,32,128]{3,2,1,0:T(8,128)S(1)} %get-tuple-element.7), channel_id=1, source_target_pairs={{0,1},{1,2},{2,3},{3,4},{4,5},{5,6},{6,7},{8,9},{9,10},{10,11},{11... | collective-permute-start | bytes 491528 | tf_op jit(solution)/shard_map/ppermute | solution.py:14
  85.7 6.6 %collective-permute-start.1 = (f32[5,2,32,128]{3,2,1,0:T(8,128)S(1)}, f32[5,2,32,128]{3,2,1,0:T(8,128)S(1)}, u32[]{:S(2)}, u32[]{:S(2)}) collective-permute-start(f32[5,2,32,128]{3,2,1,0:T(8,128)S(1)} %get-tuple-element.8), channel_id=1, source_target_pairs={{1,0},{2,1},{3,2},{4,3},{5,4},{6,5},{7,6},{9,8},{10,9},{11,10},{12... | collective-permute-start | bytes 491528 | tf_op jit(solution)/shard_map/ppermute | solution.py:15
where the time goes:
time: 95.2 us; the launch traced here: 94.6 us
  local copies, waits for them, and re-layouts  42.1 us (44%)
  waiting for transfers between devices  29 us (30%)
  starting transfers between devices  14.7 us (15%)
  other arithmetic  8.69 us (9%)
    unnamed x10, local copies, waits for them, and re-layouts  13.9 us
    all_to_all x1, waiting for transfers between devices, shards(): lax.all_to_all(fields, 'az', split_axis=1, concat_axis=3, tiled=True)  12.3 us
    gather x2, local copies, waits for them, and re-layouts, one_row(): return lax.dynamic_slice_in_dim(row, begin, length, axis=2)  12.3 us
    all_to_all x1, waiting for transfers between devices, shards(): lax.all_to_all(result, 'az', split_axis=3, concat_axis=1, tiled=True)  12 us
    concatenate x1, local copies, waits for them, and re-layouts, shards(): doubled = jnp.concatenate([block, block], axis=3)  6.97 us
    ppermute x1, starting transfers between devices, with_halo(): before = lax.ppermute(last, axis, up)  4.57 us
    ppermute x1, waiting for transfers between devices, with_halo(): after = lax.ppermute(first, axis, down)  4.4 us
    all_to_all x1, starting transfers between devices, shards(): lax.all_to_all(fields, 'az', split_axis=1, concat_axis=3, tiled=True)  4.39 us
  transfers between devices with their start and end apart: 4, of which 4 were waited for; matrix products, arithmetic and copies ran while one was open for 0% of the time, Pallas kernels for 0%

commit v1 on v0

v1 whole, which is shorter than its diff:
```python
import functools

import jax
import jax.numpy as jnp
from jax import lax
from jax.experimental import pallas as pl
from jax.experimental.pallas import tpu as pltpu
from jax.sharding import PartitionSpec as P

MESH = pl.DeviceIdType.MESH


def half_slope(left, right):
    low = jnp.maximum(jnp.minimum(left, right), 0.0)
    high = jnp.minimum(jnp.maximum(left, right), 0.0)
    return jnp.maximum(jnp.minimum(0.25 * (left + right), low), high)


def chunks_of(fields, rows, group):
    rest = rows // group - 1
    if rest == 0:
        return [(True, f, 1) for f in range(fields)]
    return [(True, 0, fields)] + [(False, f, 1) for f in range(fields)]


def kernel(
    group, rings, chunks,
    fields, shift, fraction, rates,
    out,
    own, landed, rate, bend, *rest,
):
    count = len(chunks)
    gathered, results = rest[:count], rest[count : 2 * count]
    in_sem, own_sem, send1, recv1, send2, recv2, ghost_send, ghost_recv = rest[2 * count :]
    nf, rows, polar, width = fields.shape
    me, ring = lax.axis_index("az"), lax.axis_index("rad")
    more = rows // group - 1
    start = ring * rows

    def base(first, d):
        if first:
            return jnp.where(d < 2, d, jnp.where(d < 4, rows - 4 + d, d - 2))
        return group - 2 + d * more

    def height(first):
        return 1 if first else more

    stages = [
        pltpu.make_async_copy(fields.at[:, pl.ds(0, group - 2)], own.at[:, pl.ds(0, group - 2)], in_sem.at[0]),
        pltpu.make_async_copy(fields.at[:, pl.ds(rows - 2, 2)], own.at[:, pl.ds(rows - 2, 2)], in_sem.at[1]),
    ]
    if more:
        stages.append(
            pltpu.make_async_copy(
                fields.at[:, pl.ds(group - 2, rows - group)],
                own.at[:, pl.ds(group - 2, rows - group)],
                in_sem.at[2],
            )
        )
    for copy in stages:
        copy.start()
    mine = []
    for c, (first, f0, n) in enumerate(chunks):
        copy = pltpu.make_async_copy(
            fields.at[pl.ds(f0, n), pl.ds(base(first, me), height(first))],
            gathered[c].at[me],
            own_sem.at[c],
        )
        copy.start()
        mine.append(copy)

    barrier = pltpu.get_barrier_semaphore()
    for step in range(1, group):
        pl.semaphore_signal(
            barrier, inc=1, device_id=(lax.rem(me + step, group), ring), device_id_type=MESH
        )

    @pl.when(ring > 0)
    def _():
        pl.semaphore_signal(barrier, inc=1, device_id=(me, ring - 1), device_id_type=MESH)

    @pl.when(ring < rings - 1)
    def _():
        pl.semaphore_signal(barrier, inc=1, device_id=(me, ring + 1), device_id_type=MESH)

    table = rates[...]
    place = lax.broadcasted_iota(jnp.int32, table.shape, 1)
    for j in range(rows + 1):
        column = jnp.sum(
            jnp.where(place == start - 1 + j, table, 0.0), axis=1, keepdims=True
        )
        if j == 0:
            column = jnp.where(ring > 0, column, 0.0)
        if j == rows:
            column = jnp.where(ring < rings - 1, column, 0.0)
        spread = jnp.broadcast_to(column, (polar, width))
        size = jnp.abs(spread)
        rate[j] = spread
        bend[j] = size * (1.0 - size)

    @pl.when(ring == 0)
    def _():
        landed[:, 0:2] = jnp.zeros((nf, 2, polar, width), jnp.float32)

    @pl.when(ring == rings - 1)
    def _():
        landed[:, rows + 2 : rows + 4] = jnp.zeros((nf, 2, polar, width), jnp.float32)

    neighbours = (group - 1) + jnp.where(ring > 0, 1, 0) + jnp.where(ring < rings - 1, 1, 0)
    pl.semaphore_wait(barrier, neighbours)

    def out_copy(c, d):
        first, f0, n = chunks[c]
        return pltpu.make_async_remote_copy(
            src_ref=own.at[pl.ds(f0, n), pl.ds(base(first, d), height(first))],
            dst_ref=gathered[c].at[me],
            send_sem=send1.at[c, d],
            recv_sem=recv1.at[c, me],
            device_id=(d, ring),
            device_id_type=MESH,
        )

    def in_copy(c, s):
        first, f0, n = chunks[c]
        return pltpu.make_async_remote_copy(
            src_ref=gathered[c].at[s],
            dst_ref=gathered[c].at[s],
            send_sem=send1.at[c, s],
            recv_sem=recv1.at[c, s],
            device_id=(s, ring),
            device_id_type=MESH,
        )

    def back_copy(c, d):
        first, f0, n = chunks[c]
        return pltpu.make_async_remote_copy(
            src_ref=results[c].at[d],
            dst_ref=landed.at[pl.ds(f0, n), pl.ds(2 + base(first, me), height(first))],
            send_sem=send2.at[c, d],
            recv_sem=recv2.at[c, me],
            device_id=(d, ring),
            device_id_type=MESH,
        )

    def home_copy(c, s):
        first, f0, n = chunks[c]
        target = landed.at[pl.ds(f0, n), pl.ds(2 + base(first, s), height(first))]
        return pltpu.make_async_remote_copy(
            src_ref=target,
            dst_ref=target,
            send_sem=send2.at[c, s],
            recv_sem=recv2.at[c, s],
            device_id=(s, ring),
            device_id_type=MESH,
        )

    def peers():
        return [lax.rem(me + step, group) for step in range(1, group)]

    for c in range(count):
        if c == 0:
            stages[0].wait()
            stages[1].wait()
        if c == 1 and more:
            stages[2].wait()
        for d in peers():
            out_copy(c, d).start()

    lane = lax.broadcasted_iota(jnp.int32, (polar, width), 1)
    at_first, at_last = lane == 0, lane == width - 1

    def previous(blocks):
        turned = [pltpu.roll(b, 1, 1) for b in blocks]
        return [jnp.where(at_first, turned[p - 1], turned[p]) for p in range(group)]

    def following(blocks):
        turned = [pltpu.roll(b, width - 1, 1) for b in blocks]
        return [jnp.where(at_last, turned[(p + 1) % group], turned[p]) for p in range(group)]

    cycle = group * width

    def azimuth(c):
        first, f0, n = chunks[c]
        source, target = gathered[c], results[c]
        for k in range(height(first)):
            row = start + base(first, me) + k
            courant = fraction[row]
            ahead = courant > 0.0
            amount = shift[row] + jnp.where(ahead, cycle, cycle - 1)
            whole = lax.rem(amount // width, group)
            part = lax.rem(amount, width)
            size = jnp.abs(courant)
            bent = size * (1.0 - size)
            beyond = lane >= part

            for f in range(n):
                turned = [
                    pltpu.roll(source[lax.rem(p + group - whole, group), f, k], part, 1)
                    for p in range(group)
                ]
                q = [jnp.where(beyond, turned[p], turned[p - 1]) for p in range(group)]
                before = previous(q)
                left = [x - y for x, y in zip(q, before)]
                right = following(left)
                value = [
                    courant * x + bent * half_slope(l, r) for x, l, r in zip(q, left, right)
                ]
                lower = previous(value)
                for p in range(group):
                    kept = jnp.where(ahead, q[p], before[p])
                    target[p, f, k] = kept - (value[p] - lower[p])
        landed[pl.ds(f0, n), pl.ds(2 + base(first, me), height(first))] = target[me]

    ghosts = [
        pltpu.make_async_remote_copy(
            src_ref=landed.at[:, pl.ds(2, 2)],
            dst_ref=landed.at[:, pl.ds(rows + 2, 2)],
            send_sem=ghost_send.at[0],
            recv_sem=ghost_recv.at[0],
            device_id=(me, jnp.maximum(ring - 1, 0)),
            device_id_type=MESH,
        ),
        pltpu.make_async_remote_copy(
            src_ref=landed.at[:, pl.ds(rows, 2)],
            dst_ref=landed.at[:, pl.ds(0, 2)],
            send_sem=ghost_send.at[1],
            recv_sem=ghost_recv.at[1],
            device_id=(me, jnp.minimum(ring + 1, rings - 1)),
            device_id_type=MESH,
        ),
    ]

    def radial(f):
        def cell(i):
            return landed[f, i]

        q1, q2 = cell(1), cell(2)
        d1 = q1 - cell(0)
        d2 = q2 - q1
        h1 = half_slope(d1, d2)
        below = None
        for j in range(rows + 1):
            q3 = cell(j + 3)
            d3 = q3 - q2
            h2 = half_slope(d2, d3)
            c, b = rate[j], bend[j]
            ahead = c > 0.0
            flux = c * jnp.where(ahead, q1, q2) + b * jnp.where(ahead, h1, h2)
            if j > 0:
                out[f, j - 1] = q1 - (flux - below)
            below = flux
            q1, q2, d2, h1 = q2, q3, d3, h2

    edges = 1 if more else count

    for c in range(count):
        mine[c].wait()
        for s in peers():
            in_copy(c, s).wait_recv()
        azimuth(c)
        for d in peers():
            back_copy(c, d).start()

    for c in range(edges):
        for s in peers():
            home_copy(c, s).wait_recv()

    @pl.when(ring > 0)
    def _():
        ghosts[0].start()

    @pl.when(ring < rings - 1)
    def _():
        ghosts[1].start()

    @pl.when(ring > 0)
    def _():
        ghosts[1].wait_recv()

    @pl.when(ring < rings - 1)
    def _():
        ghosts[0].wait_recv()

    for f in range(nf):
        if more:
            for s in peers():
                home_copy(edges + f, s).wait_recv()
        radial(f)

    for c in range(count):
        for d in peers():
            out_copy(c, d).wait_send()
            back_copy(c, d).wait_send()

    @pl.when(ring > 0)
    def _():
        ghosts[0].wait_send()

    @pl.when(ring < rings - 1)
    def _():
        ghosts[1].wait_send()


def shards(fields, shift, fraction, radial_rate):
    nf, rows, polar, width = fields.shape
    group, rings = lax.axis_size("az"), lax.axis_size("rad")
    chunks = chunks_of(nf, rows, group)
    more = rows // group - 1
    boxes = [
        pltpu.VMEM((group, n, 1 if first else more, polar, width), jnp.float32)
        for first, f0, n in chunks
    ]
    count = len(chunks)
    dma = pltpu.SemaphoreType.DMA
    return pl.pallas_call(
        functools.partial(kernel, group, rings, chunks),
        out_shape=jax.ShapeDtypeStruct(fields.shape, jnp.float32),
        in_specs=[
            pl.BlockSpec(memory_space=pltpu.HBM),
            pl.BlockSpec(memory_space=pltpu.SMEM),
            pl.BlockSpec(memory_space=pltpu.SMEM),
            pl.BlockSpec(memory_space=pltpu.VMEM),
        ],
        out_specs=pl.BlockSpec(memory_space=pltpu.VMEM),
        scratch_shapes=[
            pltpu.VMEM((nf, rows, polar, width), jnp.float32),
            pltpu.VMEM((nf, rows + 4, polar, width), jnp.float32),
            pltpu.VMEM((rows + 1, polar, width), jnp.float32),
            pltpu.VMEM((rows + 1, polar, width), jnp.float32),
            *boxes,
            *boxes,
            dma((3,)),
            dma((count,)),
            dma((count, group)),
            dma((count, group)),
            dma((count, group)),
            dma((count, group)),
            dma((2,)),
            dma((2,)),
        ],
        compiler_params=pltpu.CompilerParams(collective_id=0, has_side_effects=True),
    )(fields, shift, fraction, radial_rate.T)


def solution(mesh):
    placed = (P(None, "rad", None, "az"), P(), P(), P())
    return jax.shard_map(
        shards, mesh=mesh, in_specs=placed, out_specs=P(None, "rad", None, "az"), check_vma=False
    )
```

time: 95.2 us -> 32.2 us (0.34)
  the two profiles are of different devices: /device:TPU:1 before, /device:TPU:0 now
where the time goes in v1:
time: 32.2 us; the launch traced here: 31.9 us
  Pallas kernels  29.7 us (92%)
  local copies, waits for them, and re-layouts  2.24 us (7%)
    pallas_call x1, Pallas kernels, shards(): pl.pallas_call(functools.partial(kernel, group, rings, chunks), out_shape...  29.7 us
    unnamed x1, local copies, waits for them, and re-layouts  2.24 us

profile of v1, /device:TPU:0, one launch (start us, length us, event | category | flops | bytes accessed | tf_op | source)
XLA Modules:
  0.0 31.9 jit_solution(5146139567980696383)
XLA Ops:
  0.0 29.7 %shard_map.46 = f32[5,12,32,128]{3,2,1,0:T(8,128)} custom-call(f32[5,12,32,128]{3,2,1,0:T(8,128)} %fields.1, s32[96]{0:T(128)} %shift.1, f32[96]{0:T(128)} %fraction.1, f32[32,96]{1,0:T(8,128)} %bitcast.1), custom_call_target="tpu_custom_call" | custom-call | tf_op jit(solution)/shard_map/pallas_call | solution.py:315
  29.7 2.2 %copy.6 = f32[5,12,32,128]{3,2,1,0:T(8,128)} copy(f32[5,12,32,128]{3,2,1,0:T(8,128)} %shard_map.46) | data formatting | bytes 1966080

commit v2 on v1

--- a/solution.py
+++ b/solution.py
@@ -25,13 +25,13 @@
 
 def kernel(
     group, rings, chunks,
-    fields, shift, fraction, rates,
+    fields, shift_in, fraction_in, rates_in,
     out,
-    own, landed, rate, bend, *rest,
+    own, landed, rate, bend, shift, fraction, rates, *rest,
 ):
     count = len(chunks)
     gathered, results = rest[:count], rest[count : 2 * count]
-    in_sem, own_sem, send1, recv1, send2, recv2, ghost_send, ghost_recv = rest[2 * count :]
+    small_sem, in_sem, own_sem, send1, recv1, send2, recv2, ghost_send, ghost_recv = rest[2 * count :]
     nf, rows, polar, width = fields.shape
     me, ring = lax.axis_index("az"), lax.axis_index("rad")
     more = rows // group - 1
@@ -44,6 +44,14 @@
 
     def height(first):
         return 1 if first else more
+
+    small = [
+        pltpu.make_async_copy(rates_in, rates, small_sem.at[0]),
+        pltpu.make_async_copy(shift_in, shift, small_sem.at[1]),
+        pltpu.make_async_copy(fraction_in, fraction, small_sem.at[2]),
+    ]
+    for copy in small:
+        copy.start()
 
     stages = [
         pltpu.make_async_copy(fields.at[:, pl.ds(0, group - 2)], own.at[:, pl.ds(0, group - 2)], in_sem.at[0]),
@@ -83,6 +91,7 @@
     def _():
         pl.semaphore_signal(barrier, inc=1, device_id=(me, ring + 1), device_id_type=MESH)
 
+    small[0].wait()
     table = rates[...]
     place = lax.broadcasted_iota(jnp.int32, table.shape, 1)
     for j in range(rows + 1):
@@ -253,6 +262,8 @@
 
     edges = 1 if more else count
 
+    small[1].wait()
+    small[2].wait()
     for c in range(count):
         mine[c].wait()
         for s in peers():
@@ -312,23 +323,23 @@
     ]
     count = len(chunks)
     dma = pltpu.SemaphoreType.DMA
+    operands = (fields, shift, fraction, radial_rate.T)
     return pl.pallas_call(
         functools.partial(kernel, group, rings, chunks),
         out_shape=jax.ShapeDtypeStruct(fields.shape, jnp.float32),
-        in_specs=[
-            pl.BlockSpec(memory_space=pltpu.HBM),
-            pl.BlockSpec(memory_space=pltpu.SMEM),
-            pl.BlockSpec(memory_space=pltpu.SMEM),
-            pl.BlockSpec(memory_space=pltpu.VMEM),
-        ],
+        in_specs=[pl.BlockSpec(memory_space=pltpu.HBM)] * 4,
         out_specs=pl.BlockSpec(memory_space=pltpu.VMEM),
         scratch_shapes=[
             pltpu.VMEM((nf, rows, polar, width), jnp.float32),
             pltpu.VMEM((nf, rows + 4, polar, width), jnp.float32),
             pltpu.VMEM((rows + 1, polar, width), jnp.float32),
             pltpu.VMEM((rows + 1, polar, width), jnp.float32),
+            pltpu.SMEM(shift.shape, jnp.int32),
+            pltpu.SMEM(fraction.shape, jnp.float32),
+            pltpu.VMEM(radial_rate.shape[::-1], jnp.float32),
             *boxes,
             *boxes,
+            dma((3,)),
             dma((3,)),
             dma((count,)),
             dma((count, group)),
@@ -338,8 +349,10 @@
             dma((2,)),
             dma((2,)),
         ],
-        compiler_params=pltpu.CompilerParams(collective_id=0, has_side_effects=True),
-    )(fields, shift, fraction, radial_rate.T)
+        compiler_params=pltpu.CompilerParams(
+            collective_id=0, has_side_effects=True, vmem_limit_bytes=10 * fields.size * 4
+        ),
+    )(*(pltpu.with_memory_space_constraint(x, pltpu.HBM) for x in operands))
 
 
 def solution(mesh):

time: 32.2 us -> 29.4 us (0.913)
  Pallas kernels: 29.7 us -> 28.2 us
  local copies, waits for them, and re-layouts: 2.24 us -> 0.95 us
    pallas_call x1, Pallas kernels: 29.7 us -> 28.2 us  [shards(): pl.pallas_call(functools.partial(kernel, group, rings, chunks), out_shape...]
    unnamed x1, local copies, waits for them, and re-layouts: 2.24 us -> 0.95 us
where the time goes in v2:
time: 29.4 us; the launch traced here: 29.2 us
  Pallas kernels  28.2 us (96%)
  local copies, waits for them, and re-layouts  0.95 us (3%)
    pallas_call x1, Pallas kernels, shards(): pl.pallas_call(functools.partial(kernel, group, rings, chunks), out_shape...  28.2 us
    unnamed x1, local copies, waits for them, and re-layouts  0.95 us

profile of v2, /device:TPU:0, one launch (start us, length us, event | category | flops | bytes accessed | tf_op | source)
XLA Modules:
  0.0 29.2 jit_solution(6371904563477676642)
XLA Ops:
  0.0 28.2 %shard_map.46 = f32[5,12,32,128]{3,2,1,0:T(8,128)S(1)} custom-call(f32[5,12,32,128]{3,2,1,0:T(8,128)} %fields.1, s32[96]{0:T(128)} %shift_in.1, f32[96]{0:T(128)} %fraction_in.1, f32[32,96]{1,0:T(8,128)} %bitcast.1), custom_call_target="tpu_custom_call" | custom-call | tf_op jit(solution)/shard_map/pallas_call | solution.py:327
  28.2 0.9 %copy.6 = f32[5,12,32,128]{3,2,1,0:T(8,128)} copy(f32[5,12,32,128]{3,2,1,0:T(8,128)S(1)} %shard_map.46) | data formatting | bytes 1966080

commit v3 on v2

--- a/solution.py
+++ b/solution.py
@@ -21,6 +21,14 @@
     if rest == 0:
         return [(True, f, 1) for f in range(fields)]
     return [(True, 0, fields)] + [(False, f, 1) for f in range(fields)]
+
+
+def peers_of(group, me):
+    if group == 4:
+        inner = me + 1 - 2 * lax.rem(me, 2)
+        outer = lax.rem(me + 2, 4)
+        return [inner, outer], [inner + outer - me]
+    return [lax.rem(me + step, group) for step in range(1, group)], []
 
 
 def kernel(
@@ -31,7 +39,7 @@
 ):
     count = len(chunks)
     gathered, results = rest[:count], rest[count : 2 * count]
-    small_sem, in_sem, own_sem, send1, recv1, send2, recv2, ghost_send, ghost_recv = rest[2 * count :]
+    small_sem, in_sem, own_sem, send1, recv1, send2, recv2, ghost_send, ghost_recv, passed = rest[2 * count :]
     nf, rows, polar, width = fields.shape
     me, ring = lax.axis_index("az"), lax.axis_index("rad")
     more = rows // group - 1
@@ -45,13 +53,18 @@
     def height(first):
         return 1 if first else more
 
-    small = [
-        pltpu.make_async_copy(rates_in, rates, small_sem.at[0]),
-        pltpu.make_async_copy(shift_in, shift, small_sem.at[1]),
-        pltpu.make_async_copy(fraction_in, fraction, small_sem.at[2]),
-    ]
-    for copy in small:
-        copy.start()
+    near, far = peers_of(group, me)
+    barrier = pltpu.get_barrier_semaphore()
+    for d in near:
+        pl.semaphore_signal(barrier, inc=1, device_id=(d, ring), device_id_type=MESH)
+
+    @pl.when(ring > 0)
+    def _():
+        pl.semaphore_signal(barrier, inc=1, device_id=(me, ring - 1), device_id_type=MESH)
+
+    @pl.when(ring < rings - 1)
+    def _():
+        pl.semaphore_signal(barrier, inc=1, device_id=(me, ring + 1), device_id_type=MESH)
 
     stages = [
         pltpu.make_async_copy(fields.at[:, pl.ds(0, group - 2)], own.at[:, pl.ds(0, group - 2)], in_sem.at[0]),
@@ -77,19 +90,79 @@
         copy.start()
         mine.append(copy)
 
-    barrier = pltpu.get_barrier_semaphore()
-    for step in range(1, group):
-        pl.semaphore_signal(
-            barrier, inc=1, device_id=(lax.rem(me + step, group), ring), device_id_type=MESH
-        )
-
-    @pl.when(ring > 0)
-    def _():
-        pl.semaphore_signal(barrier, inc=1, device_id=(me, ring - 1), device_id_type=MESH)
-
-    @pl.when(ring < rings - 1)
-    def _():
-        pl.semaphore_signal(barrier, inc=1, device_id=(me, ring + 1), device_id_type=MESH)
+    small = [
+        pltpu.make_async_copy(rates_in, rates, small_sem.at[0]),
+        pltpu.make_async_copy(shift_in, shift, small_sem.at[1]),
+        pltpu.make_async_copy(fraction_in, fraction, small_sem.at[2]),
+    ]
+    for copy in small:
+        copy.start()
+
+    neighbours = len(near) + jnp.where(ring > 0, 1, 0) + jnp.where(ring < rings - 1, 1, 0)
+    pl.semaphore_wait(barrier, neighbours)
+    if far:
+        pl.semaphore_signal(passed, inc=1, device_id=(near[0], ring), device_id_type=MESH)
+
+    def out_copy(c, d):
+        first, f0, n = chunks[c]
+        return pltpu.make_async_remote_copy(
+            src_ref=own.at[pl.ds(f0, n), pl.ds(base(first, d), height(first))],
+            dst_ref=gathered[c].at[me],
+            send_sem=send1.at[c, d],
+            recv_sem=recv1.at[c, me],
+            device_id=(d, ring),
+            device_id_type=MESH,
+        )
+
+    def in_copy(c, s):
+        first, f0, n = chunks[c]
+        return pltpu.make_async_remote_copy(
+            src_ref=gathered[c].at[s],
+            dst_ref=gathered[c].at[s],
+            send_sem=send1.at[c, s],
+            recv_sem=recv1.at[c, s],
+            device_id=(s, ring),
+            device_id_type=MESH,
+        )
+
+    def back_copy(c, d):
+        first, f0, n = chunks[c]
+        return pltpu.make_async_remote_copy(
+            src_ref=results[c].at[d],
+            dst_ref=landed.at[pl.ds(f0, n), pl.ds(2 + base(first, me), height(first))],
+            send_sem=send2.at[c, d],
+            recv_sem=recv2.at[c, me],
+            device_id=(d, ring),
+            device_id_type=MESH,
+        )
+
+    def home_copy(c, s):
+        first, f0, n = chunks[c]
+        target = landed.at[pl.ds(f0, n), pl.ds(2 + base(first, s), height(first))]
+        return pltpu.make_async_remote_copy(
+            src_ref=target,
+            dst_ref=target,
+            send_sem=send2.at[c, s],
+            recv_sem=recv2.at[c, s],
+            device_id=(s, ring),
+            device_id_type=MESH,
+        )
+
+    def peers():
+        return far + near
+
+    for c in range(count):
+        if c == 0:
+            stages[0].wait()
+            stages[1].wait()
+        if c == 1 and more:
+            stages[2].wait()
+        for d in near:
+            out_copy(c, d).start()
+        if c == 0 and far:
+            pl.semaphore_wait(passed, 1)
+        for d in far:
+            out_copy(c, d).start()
 
     small[0].wait()
     table = rates[...]
@@ -114,66 +187,6 @@
     @pl.when(ring == rings - 1)
     def _():
         landed[:, rows + 2 : rows + 4] = jnp.zeros((nf, 2, polar, width), jnp.float32)
-
-    neighbours = (group - 1) + jnp.where(ring > 0, 1, 0) + jnp.where(ring < rings - 1, 1, 0)
-    pl.semaphore_wait(barrier, neighbours)
-
-    def out_copy(c, d):
-        first, f0, n = chunks[c]
-        return pltpu.make_async_remote_copy(
-            src_ref=own.at[pl.ds(f0, n), pl.ds(base(first, d), height(first))],
-            dst_ref=gathered[c].at[me],
-            send_sem=send1.at[c, d],
-            recv_sem=recv1.at[c, me],
-            device_id=(d, ring),
-            device_id_type=MESH,
-        )
-
-    def in_copy(c, s):
-        first, f0, n = chunks[c]
-        return pltpu.make_async_remote_copy(
-            src_ref=gathered[c].at[s],
-            dst_ref=gathered[c].at[s],
-            send_sem=send1.at[c, s],
-            recv_sem=recv1.at[c, s],
-            device_id=(s, ring),
-            device_id_type=MESH,
-        )
-
-    def back_copy(c, d):
-        first, f0, n = chunks[c]
-        return pltpu.make_async_remote_copy(
-            src_ref=results[c].at[d],
-            dst_ref=landed.at[pl.ds(f0, n), pl.ds(2 + base(first, me), height(first))],
-            send_sem=send2.at[c, d],
-            recv_sem=recv2.at[c, me],
-            device_id=(d, ring),
-            device_id_type=MESH,
-        )
-
-    def home_copy(c, s):
-        first, f0, n = chunks[c]
-        target = landed.at[pl.ds(f0, n), pl.ds(2 + base(first, s), height(first))]
-        return pltpu.make_async_remote_copy(
-            src_ref=target,
-            dst_ref=target,
-            send_sem=send2.at[c, s],
-            recv_sem=recv2.at[c, s],
-            device_id=(s, ring),
-            device_id_type=MESH,
-        )
-
-    def peers():
-        return [lax.rem(me + step, group) for step in range(1, group)]
-
-    for c in range(count):
-        if c == 0:
-            stages[0].wait()
-            stages[1].wait()
-        if c == 1 and more:
-            stages[2].wait()
-        for d in peers():
-            out_copy(c, d).start()
 
     lane = lax.broadcasted_iota(jnp.int32, (polar, width), 1)
     at_first, at_last = lane == 0, lane == width - 1
@@ -348,6 +361,7 @@
             dma((count, group)),
             dma((2,)),
             dma((2,)),
+            pltpu.SemaphoreType.REGULAR,
         ],
         compiler_params=pltpu.CompilerParams(
             collective_id=0, has_side_effects=True, vmem_limit_bytes=10 * fields.size * 4

time: 29.4 us -> 29.3 us (level)
  no operation moved by 1% of the time
where the time goes in v3:
time: 29.3 us; the launch traced here: 29.2 us
  Pallas kernels  28.2 us (96%)
  local copies, waits for them, and re-layouts  0.95 us (3%)
    pallas_call x1, Pallas kernels, shards(): pl.pallas_call(functools.partial(kernel, group, rings, chunks), out_shape...  28.2 us
    unnamed x1, local copies, waits for them, and re-layouts  0.95 us

profile of v3, /device:TPU:0, one launch (start us, length us, event | category | flops | bytes accessed | tf_op | source)
XLA Modules:
  0.0 29.2 jit_solution(850305867180587242)
XLA Ops:
  0.0 28.2 %shard_map.46 = f32[5,12,32,128]{3,2,1,0:T(8,128)S(1)} custom-call(f32[5,12,32,128]{3,2,1,0:T(8,128)} %fields.1, s32[96]{0:T(128)} %shift_in.1, f32[96]{0:T(128)} %fraction_in.1, f32[32,96]{1,0:T(8,128)} %bitcast.1), custom_call_target="tpu_custom_call" | custom-call | tf_op jit(solution)/shard_map/pallas_call | solution.py:340
  28.2 0.9 %copy.6 = f32[5,12,32,128]{3,2,1,0:T(8,128)} copy(f32[5,12,32,128]{3,2,1,0:T(8,128)S(1)} %shard_map.46) | data formatting | bytes 1966080

commit v4 on v3

--- a/solution.py
+++ b/solution.py
@@ -20,7 +20,7 @@
     rest = rows // group - 1
     if rest == 0:
         return [(True, f, 1) for f in range(fields)]
-    return [(True, 0, fields)] + [(False, f, 1) for f in range(fields)]
+    return [(True, 0, fields), (False, 0, fields - 1), (False, fields - 1, 1)]
 
 
 def peers_of(group, me):
@@ -157,11 +157,11 @@
             stages[1].wait()
         if c == 1 and more:
             stages[2].wait()
-        for d in near:
+        for d in near if c == 0 else far + near:
             out_copy(c, d).start()
         if c == 0 and far:
             pl.semaphore_wait(passed, 1)
-        for d in far:
+        for d in far if c == 0 else []:
             out_copy(c, d).start()
 
     small[0].wait()
@@ -305,11 +305,15 @@
     def _():
         ghosts[0].wait_recv()
 
-    for f in range(nf):
-        if more:
-            for s in peers():
-                home_copy(edges + f, s).wait_recv()
-        radial(f)
+    for c in range(edges, count):
+        first, f0, n = chunks[c]
+        for s in peers():
+            home_copy(c, s).wait_recv()
+        for f in range(f0, f0 + n):
+            radial(f)
+    if not more:
+        for f in range(nf):
+            radial(f)
 
     for c in range(count):
         for d in peers():

time: 29.3 us -> 28.8 us (0.983)
  Pallas kernels: 28.2 us -> 27.7 us
    pallas_call x1, Pallas kernels: 28.2 us -> 27.7 us  [shards(): pl.pallas_call(functools.partial(kernel, group, rings, chunks), out_shape...]
where the time goes in v4:
time: 28.8 us; the launch traced here: 28.7 us
  Pallas kernels  27.7 us (96%)
  local copies, waits for them, and re-layouts  0.95 us (3%)
    pallas_call x1, Pallas kernels, shards(): pl.pallas_call(functools.partial(kernel, group, rings, chunks), out_shape...  27.7 us
    unnamed x1, local copies, waits for them, and re-layouts  0.95 us

profile of v4, /device:TPU:0, one launch (start us, length us, event | category | flops | bytes accessed | tf_op | source)
XLA Modules:
  0.0 28.7 jit_solution(10026610656916541747)
XLA Ops:
  0.0 27.7 %shard_map.46 = f32[5,12,32,128]{3,2,1,0:T(8,128)S(1)} custom-call(f32[5,12,32,128]{3,2,1,0:T(8,128)} %fields.1, s32[96]{0:T(128)} %shift_in.1, f32[96]{0:T(128)} %fraction_in.1, f32[32,96]{1,0:T(8,128)} %bitcast.1), custom_call_target="tpu_custom_call" | custom-call | tf_op jit(solution)/shard_map/pallas_call | solution.py:344
  27.7 0.9 %copy.6 = f32[5,12,32,128]{3,2,1,0:T(8,128)} copy(f32[5,12,32,128]{3,2,1,0:T(8,128)S(1)} %shard_map.46) | data formatting | bytes 1966080

commit v5 on v4

--- a/solution.py
+++ b/solution.py
@@ -20,7 +20,7 @@
     rest = rows // group - 1
     if rest == 0:
         return [(True, f, 1) for f in range(fields)]
-    return [(True, 0, fields), (False, 0, fields - 1), (False, fields - 1, 1)]
+    return [(True, 0, fields), (False, 0, fields - 2), (False, fields - 2, 2)]
 
 
 def peers_of(group, me):

time: 28.8 us -> 28.6 us (level)
  no operation moved by 1% of the time
where the time goes in v5:
time: 28.6 us; the launch traced here: 28.5 us
  Pallas kernels  27.5 us (96%)
  local copies, waits for them, and re-layouts  0.95 us (3%)
    pallas_call x1, Pallas kernels, shards(): pl.pallas_call(functools.partial(kernel, group, rings, chunks), out_shape...  27.5 us
    unnamed x1, local copies, waits for them, and re-layouts  0.95 us

profile of v5, /device:TPU:0, one launch (start us, length us, event | category | flops | bytes accessed | tf_op | source)
XLA Modules:
  0.0 28.5 jit_solution(3976473482695695948)
XLA Ops:
  0.0 27.5 %shard_map.46 = f32[5,12,32,128]{3,2,1,0:T(8,128)S(1)} custom-call(f32[5,12,32,128]{3,2,1,0:T(8,128)} %fields.1, s32[96]{0:T(128)} %shift_in.1, f32[96]{0:T(128)} %fraction_in.1, f32[32,96]{1,0:T(8,128)} %bitcast.1), custom_call_target="tpu_custom_call" | custom-call | tf_op jit(solution)/shard_map/pallas_call | solution.py:344
  27.5 0.9 %copy.6 = f32[5,12,32,128]{3,2,1,0:T(8,128)} copy(f32[5,12,32,128]{3,2,1,0:T(8,128)S(1)} %shard_map.46) | data formatting | bytes 1966080

commit v6 on v5

--- a/solution.py
+++ b/solution.py
@@ -151,18 +151,25 @@
     def peers():
         return far + near
 
-    for c in range(count):
+    def ready(c):
         if c == 0:
             stages[0].wait()
             stages[1].wait()
         if c == 1 and more:
             stages[2].wait()
-        for d in near if c == 0 else far + near:
+
+    for c in range(min(2, count)):
+        ready(c)
+        for d in near:
             out_copy(c, d).start()
-        if c == 0 and far:
-            pl.semaphore_wait(passed, 1)
-        for d in far if c == 0 else []:
+    if far:
+        pl.semaphore_wait(passed, 1)
+    for c in range(count):
+        for d in far:
             out_copy(c, d).start()
+        if c > 1:
+            for d in near:
+                out_copy(c, d).start()
 
     small[0].wait()
     table = rates[...]

time: 28.6 us -> 28.6 us (level)
  no operation moved by 1% of the time
where the time goes in v6:
time: 28.6 us; the launch traced here: 28.5 us
  Pallas kernels  27.5 us (96%)
  local copies, waits for them, and re-layouts  0.95 us (3%)
    pallas_call x1, Pallas kernels, shards(): pl.pallas_call(functools.partial(kernel, group, rings, chunks), out_shape...  27.5 us
    unnamed x1, local copies, waits for them, and re-layouts  0.95 us

profile of v6, /device:TPU:0, one launch (start us, length us, event | category | flops | bytes accessed | tf_op | source)
XLA Modules:
  0.0 28.5 jit_solution(14280949964165225302)
XLA Ops:
  0.0 27.5 %shard_map.46 = f32[5,12,32,128]{3,2,1,0:T(8,128)S(1)} custom-call(f32[5,12,32,128]{3,2,1,0:T(8,128)} %fields.1, s32[96]{0:T(128)} %shift_in.1, f32[96]{0:T(128)} %fraction_in.1, f32[32,96]{1,0:T(8,128)} %bitcast.1), custom_call_target="tpu_custom_call" | custom-call | tf_op jit(solution)/shard_map/pallas_call | solution.py:351
  27.5 0.9 %copy.6 = f32[5,12,32,128]{3,2,1,0:T(8,128)} copy(f32[5,12,32,128]{3,2,1,0:T(8,128)S(1)} %shard_map.46) | data formatting | bytes 1966080
